TPU v7x, 32 devices: a whole 2x2x4 slice. The times are simulated.
32 devices in a mesh: samp: 16 (over z, y, x), tgt: 2 (over core).
Axes of the slice: x: 2, y: 2, z: 4, core: 2. Of those that a mesh axis runs over, the one named last changes fastest.
Arguments:
- samples: bfloat16 [3072, 128], P('samp'), may hold values from -6 to 6
- omega: bfloat16 [128, 4096], replicated, may hold values from -0.5 to 0.5
- phase: float32 [4096], replicated, may hold values from -3.140625 to 3.140625
- right_side: float32 [4096, 512], P('samp', 'tgt'), may hold values from -6 to 6
Outputs:
- weights: float32 [4096, 512], P('samp', 'tgt')
All inputs are finite; a program needn't handle non-finite values.
Results may differ from a plain program's by a relative error of at most 0.011.
The roundings to bfloat16 on the way count: a program that leaves them out, or rounds other values in their place, can miss the bound.
Values may be sent and summed in bfloat16 or wider, within the bound.
A program may use at most 128 MiB of HBM per device.

v0:
```python
import math
import jax
import jax.numpy as jnp
from jax import lax
from jax.sharding import PartitionSpec as P

ITERS = 2
ridge = 1.0


def precise_dot(left_matrix, right_matrix):
    return jnp.dot(left_matrix, right_matrix, precision=lax.Precision.HIGHEST)


def spd_solve(gram_matrix, rhs_matrix):
    factor = jnp.linalg.cholesky(gram_matrix)
    return jax.scipy.linalg.cho_solve((factor, True), rhs_matrix)


def cosine_block(samples, omega, phase, first_row, row_count):
    omega_cols = lax.dynamic_slice_in_dim(omega, first_row, row_count, 1)
    phase_cols = lax.dynamic_slice_in_dim(phase, first_row, row_count, 0)
    preact = jnp.dot(samples, omega_cols, preferred_element_type=jnp.float32) + phase_cols
    return jnp.cos(preact).astype(jnp.bfloat16)


def full_gram(stacked):
    summed = lax.psum(stacked, "samp")
    return lax.all_gather(summed, "tgt", axis=2, tiled=True)


def body(samples, omega, phase, right_side):
    feat_rows, col_count = right_side.shape
    samp_count = lax.axis_size("samp")
    feat_total = omega.shape[1]
    sample_total = samples.shape[0] * samp_count
    col_offset = lax.axis_index("tgt") * col_count
    store_block = math.gcd(feat_total, 512)
    stored = jnp.concatenate(
        [
            cosine_block(samples, omega, phase, index_block * store_block, store_block)
            for index_block in range(feat_total // store_block)
        ],
        axis=1,
    )

    def columns(first_row, row_count):
        return lax.dynamic_slice_in_dim(stored, first_row, row_count, 1)

    resid_all = lax.all_gather(right_side, "tgt", axis=1, tiled=True)
    direction_all = resid_all
    weight_own = jnp.zeros_like(right_side)
    gram_rr = full_gram(precise_dot(resid_all.T, right_side)[None])[0]
    for iteration in range(ITERS):
        direction_own = lax.dynamic_slice_in_dim(direction_all, col_offset, col_count, 1)
        initial = jnp.zeros((samples.shape[0], col_count), jnp.float32)
        shard_piece = lax.all_gather(direction_own.astype(jnp.bfloat16), "samp", axis=0, tiled=True)
        piece_rows = shard_piece.shape[0]
        block_size = math.gcd(piece_rows, 512)

        def project_one_block(index_block, acc_value):
            begin_row = index_block * block_size
            sub_piece = lax.dynamic_slice_in_dim(shard_piece, begin_row, block_size, 0)
            return acc_value + jnp.dot(
                columns(begin_row, block_size), sub_piece, preferred_element_type=jnp.float32
            )

        projected = lax.fori_loop(0, piece_rows // block_size, project_one_block, initial)
        proj_bf = projected.astype(jnp.bfloat16)
        transpose_row_count = feat_rows * lax.axis_size("samp")
        transpose_block_size = math.gcd(transpose_row_count, 512)

        def transpose_one_block(index_block, result):
            begin_row = index_block * transpose_block_size
            feats_block = columns(begin_row, transpose_block_size)
            block_term = lax.dot_general(
                feats_block, proj_bf, (((0,), (0,)), ((), ())), preferred_element_type=jnp.float32
            )
            return lax.dynamic_update_slice_in_dim(result, block_term, begin_row, 0)

        zero_rows = jnp.zeros((transpose_row_count, col_count), jnp.float32)
        summed_image = lax.psum_scatter(
            lax.fori_loop(
                0, transpose_row_count // transpose_block_size, transpose_one_block, zero_rows
            ),
            "samp",
            scatter_dimension=0,
            tiled=True,
        )
        image_own = summed_image / sample_total + ridge * direction_own
        image_all = lax.all_gather(image_own, "tgt", axis=1, tiled=True)
        gram_pq = full_gram(precise_dot(direction_all.T, image_own)[None])[0]
        alpha_coef = spd_solve(gram_pq, gram_rr)
        alpha_own = lax.dynamic_slice_in_dim(alpha_coef, col_offset, col_count, 1)
        weight_own = weight_own + precise_dot(direction_all, alpha_own)
        if iteration + 1 < ITERS:
            resid_all = resid_all - precise_dot(image_all, alpha_coef)
            resid_now = lax.dynamic_slice_in_dim(resid_all, col_offset, col_count, 1)
            gram_new = full_gram(precise_dot(resid_all.T, resid_now)[None])[0]
            beta_coef = spd_solve(gram_rr, gram_new)
            direction_all = resid_all + precise_dot(direction_all, beta_coef)
            gram_rr = gram_new
    return weight_own


def solution(mesh):
    placed = (P("samp", None), P(), P(), P("samp", "tgt"))
    return jax.shard_map(
        body, mesh=mesh, in_specs=placed, out_specs=P("samp", "tgt"), check_vma=False
    )
```

profile of v0, /device:TPU:0, one launch (start us, length us, event | category | flops | bytes accessed | tf_op | source)
XLA Modules:
  0.0 1215.1 jit_solution(10789328759363507932)
XLA Ops:
  22.8 50.4 %all-gather.7.cloned.1.call-done = bf16[4096,256]{1,0:T(8,128)(2,1)} async-done(((bf16[256,256]{1,0:T(8,128)(2,1)}), bf16[4096,256]{1,0:T(8,128)(2,1)}) %all-gather.7.cloned.1.call-update) | async-done | bytes 2097168 | tf_op jit(solution)/shard_map/all_gather | solution.py:57
  96.3 91.8 %reduce-scatter.3.cloned.1.call-done = f32[256,256]{1,0:T(8,128)} async-done(((f32[4096,256]{1,0:T(8,128)}), f32[256,256]{1,0:T(8,128)}) %reduce-scatter.3.cloned.1.call-update) | async-done | bytes 262160 | tf_op jit(solution)/shard_map/reduce_scatter | solution.py:82
  190.6 114.9 %all-reduce.10.cloned.1.call-done = (f32[1,512,256]{1,2,0:T(8,128)}, f32[1,512,256]{1,2,0:T(8,128)}) async-done(((f32[1,512,256]{1,2,0:T(8,128)}, f32[1,512,256]{1,2,0:T(8,128)}), (f32[1,512,256]{1,2,0:T(8,128)}, f32[1,512,256]{1,2,0:T(8,128)})) %all-reduce.10.cloned.1.call-update) | async-done | bytes 1048592 | tf_op jit(solution)/shard_map/psum | solution.py:28
  320.1 11.7 cholesky.374
  332.0 9.8 custom-call.35
  344.3 11.7 cholesky.393
  356.1 10.0 custom-call.36
  367.6 11.7 cholesky.414
  391.3 11.7 cholesky.431
  408.6 12.0 while.64
  420.6 39.3 %custom-call.38 = f32[4,128,128]{1,2,0:T(8,128)S(1)} custom-call(f32[4,128,128]{2,1,0:T(8,128)S(1)} %get-tuple-element.377), custom_call_target="InvertDiagBlocksLowerTriangular" | custom-call | tf_op jit(solution)/shard_map/jit(_cho_solve)/triangular_solve | solution.py:17
  475.0 11.7 cholesky.446
  487.5 10.8 custom-call.39
  502.1 12.5 %cholesky.465 = f32[128,128]{1,0:T(8,128)S(1)} custom-call(f32[128,128]{1,0:T(8,128)} %cholesky.603), custom_call_target="Cholesky" | custom-call | tf_op jit(solution)/shard_map/jit(cholesky)/cholesky | solution.py:16
  515.3 10.6 custom-call.40
  529.1 12.5 %cholesky.486 = f32[128,128]{1,0:T(8,128)} custom-call(f32[128,128]{1,0:T(8,128)S(1)} %cholesky.608), custom_call_target="Cholesky" | custom-call | tf_op jit(solution)/shard_map/jit(cholesky)/cholesky | solution.py:16
  543.1 10.4 custom-call.41
  555.9 12.3 %cholesky.503 = f32[128,128]{1,0:T(8,128)} custom-call(f32[128,128]{1,0:T(8,128)S(1)} %convolution_subtract_fusion.26), custom_call_target="Cholesky" | custom-call | tf_op jit(solution)/shard_map/jit(cholesky)/cholesky | solution.py:16
  578.3 105.3 %all-reduce.6.cloned.1.call-done = f32[1,512,256]{2,1,0:T(8,128)} async-done(((f32[1,512,256]{2,1,0:T(8,128)}), f32[1,512,256]{2,1,0:T(8,128)}) %all-reduce.6.cloned.1.call-update) | async-done | bytes 524304 | tf_op jit(solution)/shard_map/psum | solution.py:28
  684.4 14.8 %while.65 = (s32[]{:T(128)}, f32[512,512]{1,0:T(8,128)}, s32[4,2]{0,1:T(2,128)S(1)}, f32[4,128,128]{2,1,0:T(8,128)}, s32[]{:T(128)}) while((s32[]{:T(128)}, f32[512,512]{1,0:T(8,128)}, s32[4,2]{0,1:T(2,128)S(1)}, f32[4,128,128]{2,1,0:T(8,128)}, s32[]{:T(128)}) %tuple.227), condition=%wide.while_cond.clone, body=%wide.while_body.clone.sunk | while | flops 2 | bytes 132705 | solution.py:17
  699.2 40.8 %custom-call.42 = f32[4,128,128]{1,2,0:T(8,128)} custom-call(f32[4,128,128]{2,1,0:T(8,128)} %get-tuple-element.378), custom_call_target="InvertDiagBlocksLowerTriangular" | custom-call | tf_op jit(solution)/shard_map/jit(_cho_solve)/triangular_solve | solution.py:17
  752.9 59.5 %all-gather.15.cloned.1.call-done = bf16[4096,256]{1,0:T(8,128)(2,1)} async-done(((bf16[256,256]{1,0:T(8,128)(2,1)}), bf16[4096,256]{1,0:T(8,128)(2,1)}) %all-gather.15.cloned.1.call-update) | async-done | bytes 2097168 | tf_op jit(solution)/shard_map/all_gather | solution.py:57
  833.1 94.1 %reduce-scatter.5.cloned.1.call-done = f32[256,256]{1,0:T(8,128)} async-done(((f32[4096,256]{1,0:T(8,128)}), f32[256,256]{1,0:T(8,128)}) %reduce-scatter.5.cloned.1.call-update) | async-done | bytes 262160 | tf_op jit(solution)/shard_map/reduce_scatter | solution.py:82
  929.9 111.0 %all-reduce.8.cloned.1.call-done = f32[1,512,256]{1,2,0:T(8,128)} async-done(((f32[1,512,256]{1,2,0:T(8,128)}), f32[1,512,256]{1,2,0:T(8,128)}) %all-reduce.8.cloned.1.call-update) | async-done | bytes 524304 | tf_op jit(solution)/shard_map/psum | solution.py:28
  1055.6 11.7 cholesky.518
  1067.5 9.8 custom-call.43
  1079.8 11.7 cholesky.537
  1092.9 10.0 custom-call.44
  1104.4 11.7 cholesky.558
  1128.1 11.7 cholesky.575
  1144.4 11.5 while.66
  1155.9 39.3 %custom-call.46 = f32[4,128,128]{1,2,0:T(8,128)S(1)} custom-call(f32[4,128,128]{2,1,0:T(8,128)S(1)} %get-tuple-element.379), custom_call_target="InvertDiagBlocksLowerTriangular" | custom-call | tf_op jit(solution)/shard_map/jit(_cho_solve)/triangular_solve | solution.py:17
  (292 shorter events, 267.8 us)
Async XLA Ops:
  6.5 4.2 copy-start
  6.5 6.5 copy-start.26
  6.5 66.7 %all-gather.7.cloned.1.call-start = ((), (), s32[]{:S(2)}) async-start(), calls=%async_computation.2 | async-start | bytes 2228224 | tf_op jit(solution)/shard_map/all_gather | solution.py:57
  9.9 178.2 %reduce-scatter.3.cloned.1.call-start = ((), (), s32[]{:S(2)}) async-start(), calls=%async_computation.3 | async-start | bytes 4456448 | tf_op jit(solution)/shard_map/reduce_scatter | solution.py:82
  93.9 211.5 %all-reduce.10.cloned.1.call-start = ((), (), s32[]{:S(2)}) async-start(), calls=%async_computation.12 | async-start | bytes 2097152 | tf_op jit(solution)/shard_map/psum | solution.py:28
  190.5 124.4 %all-gather.9.cloned.1.call-start = ((), (), s32[]{:S(2)}) async-start(), calls=%async_computation.4 | async-start | bytes 1572864 | tf_op jit(solution)/shard_map/all_gather | solution.py:29
  305.5 154.5 %all-gather.11.cloned.1.call-start = ((), (), s32[]{:S(2)}) async-start(), calls=%async_computation.5 | async-start | bytes 1572864 | tf_op jit(solution)/shard_map/all_gather | solution.py:29
  307.8 375.8 %all-reduce.6.cloned.1.call-start = ((), (), s32[]{:S(2)}) async-start(), calls=%async_computation.6 | async-start | bytes 1048576 | tf_op jit(solution)/shard_map/psum | solution.py:28
  315.0 2.7 copy-start.9
  319.1 1.0 copy-start.15
  459.9 7.9 copy-start.20
  460.0 2.7 copy-start.1
  462.6 2.3 copy-start.7
  468.2 3.4 copy-start.21
  471.2 1.6 copy-start.2
  471.7 2.2 copy-start.10
  472.0 2.0 copy-start.12
  568.2 7.6 copy-start.25
  573.2 166.8 %all-gather.13.cloned.1.call-start = ((), (), s32[]{:S(2)}) async-start(), calls=%async_computation.7 | async-start | bytes 1572864 | tf_op jit(solution)/shard_map/all_gather | solution.py:29
  683.6 128.7 %all-gather.15.cloned.1.call-start = ((), (), s32[]{:S(2)}) async-start(), calls=%async_computation.8 | async-start | bytes 2228224 | tf_op jit(solution)/shard_map/all_gather | solution.py:57
  699.2 44.9 %copy-start.6 = (f32[512,512]{1,0:T(8,128)S(1)}, f32[512,512]{1,0:T(8,128)}, u32[]{:S(2)}) copy-start(f32[512,512]{1,0:T(8,128)} %get-tuple-element.842) | copy-start | bytes 3145732
  740.0 5.5 copy-start.22
  749.6 1.4 copy-start.5
  752.8 174.4 %reduce-scatter.5.cloned.1.call-start = ((), (), s32[]{:S(2)}) async-start(), calls=%async_computation.9 | async-start | bytes 4456448 | tf_op jit(solution)/shard_map/reduce_scatter | solution.py:82
  833.0 207.9 %copy-start.3 = (f32[128,512]{1,0:T(8,128)S(1)}, f32[128,512]{1,0:T(8,128)}, u32[]{:S(2)}) copy-start(f32[128,512]{1,0:T(8,128)} %copy-done.2) | copy-start | bytes 786436
  833.0 207.9 %copy-start.13 = (f32[128,512]{1,0:T(8,128)S(1)}, f32[128,512]{1,0:T(8,128)}, u32[]{:S(2)}) copy-start(f32[128,512]{1,0:T(8,128)} %copy-done.12) | copy-start | bytes 786436
  833.0 207.9 %copy-start.18 = (f32[128,512]{1,0:T(8,128)S(1)}, f32[128,512]{1,0:T(8,128)}, u32[]{:S(2)}) copy-start(f32[128,512]{1,0:T(8,128)} %fusion.170) | copy-start | bytes 786436
  833.0 207.9 %all-reduce.8.cloned.1.call-start = ((), (), s32[]{:S(2)}) async-start(), calls=%async_computation.10 | async-start | bytes 1048576 | tf_op jit(solution)/shard_map/psum | solution.py:28
  929.7 120.8 %all-gather.17.cloned.1.call-start = ((), (), s32[]{:S(2)}) async-start(), calls=%async_computation.11 | async-start | bytes 1572864 | tf_op jit(solution)/shard_map/all_gather | solution.py:29
  1050.5 2.7 copy-start.11
  1155.9 42.5 %copy-start.8 = (f32[512,512]{1,0:T(8,128)S(1)}, f32[512,512]{1,0:T(8,128)}, u32[]{:S(2)}) copy-start(f32[512,512]{1,0:T(8,128)} %get-tuple-element.844) | copy-start | bytes 3145732
  1204.9 1.4 copy-start.17
  (6 other events, 5.1 us)
Sparse Core Ops, SparseCore 0:
  10.1 63.1 all-gather.6
  94.0 94.0 reduce-scatter.2
  193.4 111.9 all-reduce.9
  306.8 8.0 all-gather.8
  316.4 10.1 all-gather.10
  573.3 110.2 all-reduce.5
  685.2 8.0 all-gather.12
  752.9 59.3 all-gather.14
  833.1 94.0 reduce-scatter.4
  932.2 108.6 all-reduce.7
  1042.4 8.0 all-gather.16
where the time goes:
time: 1230 us; the launch traced here: 1220 us
  waiting for transfers between devices  643 us (52%)
  other arithmetic  372 us (30%)
  matrix products  111 us (9%)
  local copies, waits for them, and re-layouts  60.6 us (5%)
  between operations  22.3 us (2%)
    psum x3, waiting for transfers between devices, full_gram(): summed = lax.psum(stacked, 'samp')  331 us
    another operation x43, other arithmetic, spd_solve(): factor = jnp.linalg.cholesky(gram_matrix)  243 us
    reduce_scatter x2, waiting for transfers between devices, body(): lax.psum_scatter(lax.fori_loop(0, transpose_row_count // transpose_block_...  186 us
    another operation x8, other arithmetic, spd_solve(): return jax.scipy.linalg.cho_solve((factor, True), rhs_matrix)  124 us
    all_gather x2, waiting for transfers between devices, body(): lax.all_gather(direction_own.astype(jnp.bfloat16), 'samp', axis=0, tiled=...  110 us
    another operation x40, local copies, waits for them, and re-layouts, spd_solve(): return jax.scipy.linalg.cho_solve((factor, True), rhs_matrix)  38.5 us
    another operation x42, matrix products, spd_solve(): return jax.scipy.linalg.cho_solve((factor, True), rhs_matrix)  31.8 us
  transfers between devices with their start and end apart: 11, of which 9 were waited for; matrix products, arithmetic and copies ran while one was open for 18% of the time, Pallas kernels for 0%

commit v1 on v0

--- a/solution.py
+++ b/solution.py
@@ -25,7 +25,9 @@
 
 
 def full_gram(stacked):
-    summed = lax.psum(stacked, "samp")
+    summed = stacked
+    for hop in (1, 2, 4, 8):
+        summed = summed + lax.ppermute(summed, "samp", [(dev, dev ^ hop) for dev in range(16)])
     return lax.all_gather(summed, "tgt", axis=2, tiled=True)
 
 

time: 1230 us -> 1060 us (0.86)
  waiting for transfers between devices: 643 us -> 446 us
  starting transfers between devices: 0.93 us -> 22.5 us
  other arithmetic: 372 us -> 392 us
    psum x3 -> x0, waiting for transfers between devices: 331 us -> none  [full_gram(): summed = lax.psum(stacked, 'samp')]
    ppermute x0 -> x16, waiting for transfers between devices: none -> 170 us  [full_gram(): lax.ppermute(summed, 'samp', [(dev, dev ^ hop) for dev in range(16)])]
    reduce_scatter x2, waiting for transfers between devices: 186 us -> 158 us  [body(): lax.psum_scatter(lax.fori_loop(0, transpose_row_count // transpose_block_...]
    ppermute x0 -> x16, starting transfers between devices: none -> 21.8 us  [full_gram(): lax.ppermute(summed, 'samp', [(dev, dev ^ hop) for dev in range(16)])]
    add x0 -> x16, other arithmetic: none -> 13.7 us  [full_gram(): summed + lax.ppermute(summed, 'samp', [(dev, dev ^ hop) for dev in range(...]
  transfers between devices with their start and end apart: 11 -> 24, of which waited for: 9 -> 17; matrix products, arithmetic and copies ran while one was open for 18% -> 16% of each run, Pallas kernels for 0% -> 0%
where the time goes in v1:
time: 1060 us; the launch traced here: 1050 us
  waiting for transfers between devices  446 us (42%)
  other arithmetic  392 us (37%)
  matrix products  103 us (10%)
  local copies, waits for them, and re-layouts  58.7 us (6%)
  between operations  23.9 us (2%)
  starting transfers between devices  22.5 us (2%)
    another operation x43, other arithmetic, spd_solve(): factor = jnp.linalg.cholesky(gram_matrix)  247 us
    ppermute x16, waiting for transfers between devices, full_gram(): lax.ppermute(summed, 'samp', [(dev, dev ^ hop) for dev in range(16)])  170 us
    reduce_scatter x2, waiting for transfers between devices, body(): lax.psum_scatter(lax.fori_loop(0, transpose_row_count // transpose_block_...  158 us
    another operation x8, other arithmetic, spd_solve(): return jax.scipy.linalg.cho_solve((factor, True), rhs_matrix)  126 us
    all_gather x2, waiting for transfers between devices, body(): lax.all_gather(direction_own.astype(jnp.bfloat16), 'samp', axis=0, tiled=...  110 us
    another operation x40, local copies, waits for them, and re-layouts, spd_solve(): return jax.scipy.linalg.cho_solve((factor, True), rhs_matrix)  33.5 us
    another operation x42, matrix products, spd_solve(): return jax.scipy.linalg.cho_solve((factor, True), rhs_matrix)  27.5 us
    ppermute x16, starting transfers between devices, full_gram(): lax.ppermute(summed, 'samp', [(dev, dev ^ hop) for dev in range(16)])  21.8 us
  transfers between devices with their start and end apart: 24, of which 17 were waited for; matrix products, arithmetic and copies ran while one was open for 16% of the time, Pallas kernels for 0%

profile of v1, /device:TPU:0, one launch (start us, length us, event | category | flops | bytes accessed | tf_op | source)
XLA Modules:
  0.0 1052.7 jit_solution(5057444541233907732)
XLA Ops:
  23.6 50.4 %all-gather.7.cloned.1.call-done = bf16[4096,256]{1,0:T(8,128)(2,1)} async-done(((bf16[256,256]{1,0:T(8,128)(2,1)}), bf16[4096,256]{1,0:T(8,128)(2,1)}) %all-gather.7.cloned.1.call-update) | async-done | bytes 2097168 | tf_op jit(solution)/shard_map/all_gather | solution.py:59
  97.7 32.0 %collective-permute-done.4 = f32[1,512,256]{1,2,0:T(8,128)S(1)} collective-permute-done((f32[1,512,256]{1,2,0:T(8,128)S(1)}, f32[1,512,256]{1,2,0:T(8,128)S(1)}, u32[]{:S(2)}, u32[]{:S(2)}) %collective-permute-start.4) | collective-permute-done | bytes 524320 | tf_op jit(solution)/shard_map/ppermute | solution.py:30
  130.8 63.8 %reduce-scatter.3.cloned.1.call-done = f32[256,256]{1,0:T(8,128)} async-done(((f32[4096,256]{1,0:T(8,128)}), f32[256,256]{1,0:T(8,128)}) %reduce-scatter.3.cloned.1.call-update) | async-done | bytes 262160 | tf_op jit(solution)/shard_map/reduce_scatter | solution.py:84
  226.3 12.7 %collective-permute-done.7 = f32[1,512,256]{1,2,0:T(8,128)S(1)} collective-permute-done((f32[1,512,256]{1,2,0:T(8,128)S(1)}, f32[1,512,256]{1,2,0:T(8,128)S(1)}, u32[]{:S(2)}, u32[]{:S(2)}) %collective-permute-start.7) | collective-permute-done | bytes 524320 | tf_op jit(solution)/shard_map/ppermute | solution.py:30
  248.3 23.4 %collective-permute-done.3 = f32[1,512,256]{1,2,0:T(8,128)S(1)} collective-permute-done((f32[1,512,256]{1,2,0:T(8,128)S(1)}, f32[1,512,256]{1,2,0:T(8,128)S(1)}, u32[]{:S(2)}, u32[]{:S(2)}) %collective-permute-start.3) | collective-permute-done | bytes 524320 | tf_op jit(solution)/shard_map/ppermute | solution.py:30
  278.4 12.5 %cholesky.446 = f32[128,128]{1,0:T(8,128)S(1)} custom-call(f32[128,128]{1,0:T(8,128)} %cholesky.599), custom_call_target="Cholesky" | custom-call | tf_op jit(solution)/shard_map/jit(cholesky)/cholesky | solution.py:16
  291.6 11.3 %custom-call.39 = f32[1,128,128]{1,2,0:T(8,128)} custom-call(f32[1,128,128]{2,1,0:T(8,128)} %get-tuple-element.461), custom_call_target="InvertDiagBlocksLowerTriangular" | custom-call | tf_op jit(solution)/shard_map/jit(cholesky)/cholesky | solution.py:16
  311.8 11.7 %cholesky.374 = f32[128,128]{1,0:T(8,128)S(1)} custom-call(f32[128,128]{1,0:T(8,128)S(1)} %cholesky.586), custom_call_target="Cholesky" | custom-call | tf_op jit(solution)/shard_map/jit(cholesky)/cholesky | solution.py:16
  337.7 11.7 %cholesky.393 = f32[128,128]{1,0:T(8,128)S(1)} custom-call(f32[128,128]{1,0:T(8,128)S(1)} %cholesky.590), custom_call_target="Cholesky" | custom-call | tf_op jit(solution)/shard_map/jit(cholesky)/cholesky | solution.py:16
  350.0 10.2 custom-call.36
  362.7 11.7 %cholesky.414 = f32[128,128]{1,0:T(8,128)S(1)} custom-call(f32[128,128]{1,0:T(8,128)S(1)} %cholesky.595), custom_call_target="Cholesky" | custom-call | tf_op jit(solution)/shard_map/jit(cholesky)/cholesky | solution.py:16
  387.7 11.7 %cholesky.431 = f32[128,128]{1,0:T(8,128)S(1)} custom-call(f32[128,128]{1,0:T(8,128)S(1)} %convolution_subtract_fusion.24), custom_call_target="Cholesky" | custom-call | tf_op jit(solution)/shard_map/jit(cholesky)/cholesky | solution.py:16
  406.5 11.5 %while.64 = (s32[]{:T(128)}, f32[512,512]{1,0:T(8,128)}, s32[4,2]{0,1:T(2,128)S(1)}, f32[4,128,128]{2,1,0:T(8,128)S(1)}, s32[]{:T(128)}) while((s32[]{:T(128)}, f32[512,512]{1,0:T(8,128)}, s32[4,2]{0,1:T(2,128)S(1)}, f32[4,128,128]{2,1,0:T(8,128)S(1)}, s32[]{:T(128)}) %tuple.186), condition=%wide.while_cond, body=%wide.while_body.sunk | while | flops 2 | bytes 131181 | solution.py:17
  418.7 40.1 %custom-call.38 = f32[4,128,128]{1,2,0:T(8,128)S(1)} custom-call(f32[4,128,128]{2,1,0:T(8,128)} %copy-done.28), custom_call_target="InvertDiagBlocksLowerTriangular" | custom-call | tf_op jit(solution)/shard_map/jit(_cho_solve)/triangular_solve | solution.py:17
  475.6 12.9 %cholesky.465 = f32[128,128]{1,0:T(8,128)S(1)} custom-call(f32[128,128]{1,0:T(8,128)} %cholesky.603), custom_call_target="Cholesky" | custom-call | tf_op jit(solution)/shard_map/jit(cholesky)/cholesky | solution.py:16
  489.1 10.6 %custom-call.40 = f32[1,128,128]{1,2,0:T(8,128)S(1)} custom-call(f32[1,128,128]{2,1,0:T(8,128)} %get-tuple-element.458), custom_call_target="InvertDiagBlocksLowerTriangular" | custom-call | tf_op jit(solution)/shard_map/jit(cholesky)/cholesky | solution.py:16
  505.1 12.5 %cholesky.486 = f32[128,128]{1,0:T(8,128)S(1)} custom-call(f32[128,128]{1,0:T(8,128)} %cholesky.608), custom_call_target="Cholesky" | custom-call | tf_op jit(solution)/shard_map/jit(cholesky)/cholesky | solution.py:16
  518.3 10.6 %custom-call.41 = f32[1,128,128]{1,2,0:T(8,128)S(1)} custom-call(f32[1,128,128]{2,1,0:T(8,128)} %get-tuple-element.455), custom_call_target="InvertDiagBlocksLowerTriangular" | custom-call | tf_op jit(solution)/shard_map/jit(cholesky)/cholesky | solution.py:16
  532.5 12.5 %cholesky.503 = f32[128,128]{1,0:T(8,128)} custom-call(f32[128,128]{1,0:T(8,128)S(1)} %convolution_subtract_fusion.23), custom_call_target="Cholesky" | custom-call | tf_op jit(solution)/shard_map/jit(cholesky)/cholesky | solution.py:16
  554.7 21.5 %collective-permute-done.11 = f32[1,512,256]{2,1,0:T(8,128)} collective-permute-done((f32[1,512,256]{2,1,0:T(8,128)}, f32[1,512,256]{2,1,0:T(8,128)}, u32[]{:S(2)}, u32[]{:S(2)}) %collective-permute-start.11) | collective-permute-done | bytes 524320 | tf_op jit(solution)/shard_map/ppermute | solution.py:30
  589.0 40.7 %custom-call.42 = f32[4,128,128]{1,2,0:T(8,128)} custom-call(f32[4,128,128]{2,1,0:T(8,128)} %get-tuple-element.378), custom_call_target="InvertDiagBlocksLowerTriangular" | custom-call | tf_op jit(solution)/shard_map/jit(_cho_solve)/triangular_solve | solution.py:17
  640.7 59.1 %all-gather.15.cloned.1.call-done = bf16[4096,256]{1,0:T(8,128)(2,1)} async-done(((bf16[256,256]{1,0:T(8,128)(2,1)}), bf16[4096,256]{1,0:T(8,128)(2,1)}) %all-gather.15.cloned.1.call-update) | async-done | bytes 2097168 | tf_op jit(solution)/shard_map/all_gather | solution.py:59
  720.7 93.9 %reduce-scatter.5.cloned.1.call-done = f32[256,256]{1,0:T(8,128)} async-done(((f32[4096,256]{1,0:T(8,128)}), f32[256,256]{1,0:T(8,128)}) %reduce-scatter.5.cloned.1.call-update) | async-done | bytes 262160 | tf_op jit(solution)/shard_map/reduce_scatter | solution.py:84
  816.3 12.8 %collective-permute-done.12 = f32[1,512,256]{1,2,0:T(8,128)S(1)} collective-permute-done((f32[1,512,256]{1,2,0:T(8,128)S(1)}, f32[1,512,256]{1,2,0:T(8,128)S(1)}, u32[]{:S(2)}, u32[]{:S(2)}) %collective-permute-start.12) | collective-permute-done | bytes 524320 | tf_op jit(solution)/shard_map/ppermute | solution.py:30
  829.3 11.9 %collective-permute-done.13 = f32[1,512,256]{1,2,0:T(8,128)S(1)} collective-permute-done((f32[1,512,256]{1,2,0:T(8,128)S(1)}, f32[1,512,256]{1,2,0:T(8,128)S(1)}, u32[]{:S(2)}, u32[]{:S(2)}) %collective-permute-start.13) | collective-permute-done | bytes 524320 | tf_op jit(solution)/shard_map/ppermute | solution.py:30
  856.6 20.1 %collective-permute-done.15 = f32[1,512,256]{1,2,0:T(8,128)S(1)} collective-permute-done((f32[1,512,256]{1,2,0:T(8,128)S(1)}, f32[1,512,256]{1,2,0:T(8,128)S(1)}, u32[]{:S(2)}, u32[]{:S(2)}) %collective-permute-start.15) | collective-permute-done | bytes 524320 | tf_op jit(solution)/shard_map/ppermute | solution.py:30
  892.5 11.7 %cholesky.518 = f32[128,128]{1,0:T(8,128)S(1)} custom-call(f32[128,128]{1,0:T(8,128)S(1)} %cholesky.612), custom_call_target="Cholesky" | custom-call | tf_op jit(solution)/shard_map/jit(cholesky)/cholesky | solution.py:16
  916.7 12.1 %cholesky.537 = f32[128,128]{1,0:T(8,128)S(1)} custom-call(f32[128,128]{1,0:T(8,128)S(1)} %cholesky.616), custom_call_target="Cholesky" | custom-call | tf_op jit(solution)/shard_map/jit(cholesky)/cholesky | solution.py:16
  941.5 11.7 %cholesky.558 = f32[128,128]{1,0:T(8,128)S(1)} custom-call(f32[128,128]{1,0:T(8,128)S(1)} %cholesky.621), custom_call_target="Cholesky" | custom-call | tf_op jit(solution)/shard_map/jit(cholesky)/cholesky | solution.py:16
  965.2 11.9 %cholesky.575 = f32[128,128]{1,0:T(8,128)S(1)} custom-call(f32[128,128]{1,0:T(8,128)S(1)} %convolution_subtract_fusion.22), custom_call_target="Cholesky" | custom-call | tf_op jit(solution)/shard_map/jit(cholesky)/cholesky | solution.py:16
  981.4 11.5 %while.66 = (s32[]{:T(128)}, f32[512,512]{1,0:T(8,128)}, s32[4,2]{0,1:T(2,128)S(1)}, f32[4,128,128]{2,1,0:T(8,128)S(1)}, s32[]{:T(128)}) while((s32[]{:T(128)}, f32[512,512]{1,0:T(8,128)}, s32[4,2]{0,1:T(2,128)S(1)}, f32[4,128,128]{2,1,0:T(8,128)S(1)}, s32[]{:T(128)}) %tuple.222), condition=%wide.while_cond.clone.1, body=%wide.while_body.clone.1.sunk | while | flops 2 | bytes 131181 | solution.py:17
  992.9 39.3 %custom-call.46 = f32[4,128,128]{1,2,0:T(8,128)S(1)} custom-call(f32[4,128,128]{2,1,0:T(8,128)S(1)} %get-tuple-element.379), custom_call_target="InvertDiagBlocksLowerTriangular" | custom-call | tf_op jit(solution)/shard_map/jit(_cho_solve)/triangular_solve | solution.py:17
  (341 shorter events, 365.7 us)
Async XLA Ops:
  7.4 6.5 copy-start.31
  7.4 66.7 %all-gather.7.cloned.1.call-start = ((), (), s32[]{:S(2)}) async-start(), calls=%async_computation.2 | async-start | bytes 2228224 | tf_op jit(solution)/shard_map/all_gather | solution.py:59
  10.7 183.9 %reduce-scatter.3.cloned.1.call-start = ((), (), s32[]{:S(2)}) async-start(), calls=%async_computation.3 | async-start | bytes 4456448 | tf_op jit(solution)/shard_map/reduce_scatter | solution.py:84
  94.8 177.9 %all-gather.11.cloned.1.call-start = ((), (), s32[]{:S(2)}) async-start(), calls=%async_computation.5 | async-start | bytes 1572864 | tf_op jit(solution)/shard_map/all_gather | solution.py:31
  96.3 33.3 %collective-permute-start.4 = (f32[1,512,256]{1,2,0:T(8,128)S(1)}, f32[1,512,256]{1,2,0:T(8,128)S(1)}, u32[]{:S(2)}, u32[]{:S(2)}) collective-permute-start(f32[1,512,256]{1,2,0:T(8,128)S(1)} %convolution_bitcast_fusion.3), channel_id=1, source_target_pairs={{0,2},{2,0},{4,6},{6,4},{8,10},{10,8},{12,14},{14,12},{16,18},{18,... | collective-permute-start | bytes 1572872 | tf_op jit(solution)/shard_map/ppermute | solution.py:30
  129.7 67.8 %collective-permute-start.5 = (f32[1,512,256]{1,2,0:T(8,128)S(1)}, f32[1,512,256]{1,2,0:T(8,128)}, u32[]{:S(2)}, u32[]{:S(2)}) collective-permute-start(f32[1,512,256]{1,2,0:T(8,128)S(1)} %add.301), channel_id=1, source_target_pairs={{0,4},{2,6},{4,0},{6,2},{8,12},{10,14},{12,8},{14,10},{16,20},{18,... | collective-permute-start | bytes 1572872 | tf_op jit(solution)/shard_map/ppermute | solution.py:30
  196.2 13.4 %collective-permute-start = (f32[1,512,256]{1,2,0:T(8,128)S(1)}, f32[1,512,256]{1,2,0:T(8,128)S(1)}, u32[]{:S(2)}, u32[]{:S(2)}) collective-permute-start(f32[1,512,256]{1,2,0:T(8,128)S(1)} %convolution_bitcast_fusion.4), channel_id=1, source_target_pairs={{0,2},{2,0},{4,6},{6,4},{8,10},{10,8},{12,14},{14,12},{16,18},{18,... | collective-permute-start | bytes 1572872 | tf_op jit(solution)/shard_map/ppermute | solution.py:30
  198.7 15.1 %collective-permute-start.6 = (f32[1,512,256]{1,2,0:T(8,128)S(1)}, f32[1,512,256]{1,2,0:T(8,128)S(1)}, u32[]{:S(2)}, u32[]{:S(2)}) collective-permute-start(f32[1,512,256]{1,2,0:T(8,128)S(1)} %add.302), channel_id=1, source_target_pairs={{0,8},{2,10},{4,12},{6,14},{8,0},{10,2},{12,4},{14,6},{16,24},{18,... | collective-permute-start | bytes 1572872 | tf_op jit(solution)/shard_map/ppermute | solution.py:30
  209.7 13.2 %collective-permute-start.1 = (f32[1,512,256]{1,2,0:T(8,128)S(1)}, f32[1,512,256]{1,2,0:T(8,128)S(1)}, u32[]{:S(2)}, u32[]{:S(2)}) collective-permute-start(f32[1,512,256]{1,2,0:T(8,128)S(1)} %add.297), channel_id=1, source_target_pairs={{0,4},{2,6},{4,0},{6,2},{8,12},{10,14},{12,8},{14,10},{16,20},{18,... | collective-permute-start | bytes 1572872 | tf_op jit(solution)/shard_map/ppermute | solution.py:30
  213.9 25.1 %collective-permute-start.7 = (f32[1,512,256]{1,2,0:T(8,128)S(1)}, f32[1,512,256]{1,2,0:T(8,128)S(1)}, u32[]{:S(2)}, u32[]{:S(2)}) collective-permute-start(f32[1,512,256]{1,2,0:T(8,128)S(1)} %add.303), channel_id=1, source_target_pairs={{0,16},{2,18},{4,20},{6,22},{8,24},{10,26},{12,28},{14,30},{16,0},... | collective-permute-start | bytes 1572872 | tf_op jit(solution)/shard_map/ppermute | solution.py:30
  223.0 24.2 %collective-permute-start.2 = (f32[1,512,256]{1,2,0:T(8,128)S(1)}, f32[1,512,256]{1,2,0:T(8,128)}, u32[]{:S(2)}, u32[]{:S(2)}) collective-permute-start(f32[1,512,256]{1,2,0:T(8,128)S(1)} %add.298), channel_id=1, source_target_pairs={{0,8},{2,10},{4,12},{6,14},{8,0},{10,2},{12,4},{14,6},{16,24},{18,... | collective-permute-start | bytes 1572872 | tf_op jit(solution)/shard_map/ppermute | solution.py:30
  239.9 66.6 %all-gather.9.cloned.1.call-start = ((), (), s32[]{:S(2)}) async-start(), calls=%async_computation.4 | async-start | bytes 1572864 | tf_op jit(solution)/shard_map/all_gather | solution.py:31
  248.3 23.4 %collective-permute-start.3 = (f32[1,512,256]{1,2,0:T(8,128)S(1)}, f32[1,512,256]{1,2,0:T(8,128)S(1)}, u32[]{:S(2)}, u32[]{:S(2)}) collective-permute-start(f32[1,512,256]{1,2,0:T(8,128)S(1)} %add.299), channel_id=1, source_target_pairs={{0,16},{2,18},{4,20},{6,22},{8,24},{10,26},{12,28},{14,30},{16,0},... | collective-permute-start | bytes 1572872 | tf_op jit(solution)/shard_map/ppermute | solution.py:30
  272.6 357.1 %all-gather.13.cloned.1.call-start = ((), (), s32[]{:S(2)}) async-start(), calls=%async_computation.6 | async-start | bytes 1572864 | tf_op jit(solution)/shard_map/all_gather | solution.py:31
  470.5 29.3 %collective-permute-start.8 = (f32[1,512,256]{2,1,0:T(8,128)}, f32[1,512,256]{2,1,0:T(8,128)}, u32[]{:S(2)}, u32[]{:S(2)}) collective-permute-start(f32[1,512,256]{2,1,0:T(8,128)} %convolution_bitcast_fusion.2), channel_id=1, source_target_pairs={{0,2},{2,0},{4,6},{6,4},{8,10},{10,8},{12,14},{14,12},{16,18},{18,... | collective-permute-start | bytes 1572872 | tf_op jit(solution)/shard_map/ppermute | solution.py:30
  501.9 27.0 %collective-permute-start.9 = (f32[1,512,256]{2,1,0:T(8,128)}, f32[1,512,256]{2,1,0:T(8,128)}, u32[]{:S(2)}, u32[]{:S(2)}) collective-permute-start(f32[1,512,256]{2,1,0:T(8,128)} %add.305), channel_id=1, source_target_pairs={{0,4},{2,6},{4,0},{6,2},{8,12},{10,14},{12,8},{14,10},{16,20},{18,... | collective-permute-start | bytes 1572872 | tf_op jit(solution)/shard_map/ppermute | solution.py:30
  531.0 16.9 %collective-permute-start.10 = (f32[1,512,256]{2,1,0:T(8,128)}, f32[1,512,256]{2,1,0:T(8,128)}, u32[]{:S(2)}, u32[]{:S(2)}) collective-permute-start(f32[1,512,256]{2,1,0:T(8,128)} %add.306), channel_id=1, source_target_pairs={{0,8},{2,10},{4,12},{6,14},{8,0},{10,2},{12,4},{14,6},{16,24},{18,... | collective-permute-start | bytes 1572872 | tf_op jit(solution)/shard_map/ppermute | solution.py:30
  545.0 7.3 copy-start.30
  550.0 26.1 %collective-permute-start.11 = (f32[1,512,256]{2,1,0:T(8,128)}, f32[1,512,256]{2,1,0:T(8,128)}, u32[]{:S(2)}, u32[]{:S(2)}) collective-permute-start(f32[1,512,256]{2,1,0:T(8,128)} %add.307), channel_id=1, source_target_pairs={{0,16},{2,18},{4,20},{6,22},{8,24},{10,26},{12,28},{14,30},{16,0},... | collective-permute-start | bytes 1572872 | tf_op jit(solution)/shard_map/ppermute | solution.py:30
  554.7 24.3 %copy-start.9 = (f32[512,512]{1,0:T(8,128)S(1)}, f32[512,512]{1,0:T(8,128)}, u32[]{:S(2)}) copy-start(f32[512,512]{1,0:T(8,128)} %select_select_fusion.1) | copy-start | bytes 3145732
  578.2 121.5 %all-gather.15.cloned.1.call-start = ((), (), s32[]{:S(2)}) async-start(), calls=%async_computation.7 | async-start | bytes 2228224 | tf_op jit(solution)/shard_map/all_gather | solution.py:59
  629.7 4.5 copy-start.23
  640.6 174.0 %reduce-scatter.5.cloned.1.call-start = ((), (), s32[]{:S(2)}) async-start(), calls=%async_computation.8 | async-start | bytes 4456448 | tf_op jit(solution)/shard_map/reduce_scatter | solution.py:84
  720.4 167.0 %all-gather.17.cloned.1.call-start = ((), (), s32[]{:S(2)}) async-start(), calls=%async_computation.9 | async-start | bytes 1572864 | tf_op jit(solution)/shard_map/all_gather | solution.py:31
  816.3 12.9 %collective-permute-start.12 = (f32[1,512,256]{1,2,0:T(8,128)S(1)}, f32[1,512,256]{1,2,0:T(8,128)S(1)}, u32[]{:S(2)}, u32[]{:S(2)}) collective-permute-start(f32[1,512,256]{1,2,0:T(8,128)S(1)} %convolution_bitcast_fusion), channel_id=1, source_target_pairs={{0,2},{2,0},{4,6},{6,4},{8,10},{10,8},{12,14},{14,12},{16,18},{18,... | collective-permute-start | bytes 1572872 | tf_op jit(solution)/shard_map/ppermute | solution.py:30
  829.2 12.0 %collective-permute-start.13 = (f32[1,512,256]{1,2,0:T(8,128)S(1)}, f32[1,512,256]{1,2,0:T(8,128)S(1)}, u32[]{:S(2)}, u32[]{:S(2)}) collective-permute-start(f32[1,512,256]{1,2,0:T(8,128)S(1)} %add.311), channel_id=1, source_target_pairs={{0,4},{2,6},{4,0},{6,2},{8,12},{10,14},{12,8},{14,10},{16,20},{18,... | collective-permute-start | bytes 1572872 | tf_op jit(solution)/shard_map/ppermute | solution.py:30
  841.3 36.2 %copy-start.5 = (f32[128,512]{1,0:T(8,128)S(1)}, f32[128,512]{1,0:T(8,128)}, u32[]{:S(2)}) copy-start(f32[128,512]{1,0:T(8,128)} %copy-done.4) | copy-start | bytes 786436
  841.3 36.2 %copy-start.14 = (f32[128,512]{1,0:T(8,128)S(1)}, f32[128,512]{1,0:T(8,128)}, u32[]{:S(2)}) copy-start(f32[128,512]{1,0:T(8,128)} %copy-done.13) | copy-start | bytes 786436
  841.4 36.2 %copy-start.20 = (f32[128,512]{1,0:T(8,128)S(1)}, f32[128,512]{1,0:T(8,128)}, u32[]{:S(2)}) copy-start(f32[128,512]{1,0:T(8,128)} %copy-done.19) | copy-start | bytes 786436
  841.4 11.8 %collective-permute-start.14 = (f32[1,512,256]{1,2,0:T(8,128)S(1)}, f32[1,512,256]{1,2,0:T(8,128)S(1)}, u32[]{:S(2)}, u32[]{:S(2)}) collective-permute-start(f32[1,512,256]{1,2,0:T(8,128)S(1)} %add.312), channel_id=1, source_target_pairs={{0,8},{2,10},{4,12},{6,14},{8,0},{10,2},{12,4},{14,6},{16,24},{18,... | collective-permute-start | bytes 1572872 | tf_op jit(solution)/shard_map/ppermute | solution.py:30
  853.3 23.4 %collective-permute-start.15 = (f32[1,512,256]{1,2,0:T(8,128)S(1)}, f32[1,512,256]{1,2,0:T(8,128)S(1)}, u32[]{:S(2)}, u32[]{:S(2)}) collective-permute-start(f32[1,512,256]{1,2,0:T(8,128)S(1)} %add.313), channel_id=1, source_target_pairs={{0,16},{2,18},{4,20},{6,22},{8,24},{10,26},{12,28},{14,30},{16,0},... | collective-permute-start | bytes 1572872 | tf_op jit(solution)/shard_map/ppermute | solution.py:30
  992.9 42.5 %copy-start.10 = (f32[512,512]{1,0:T(8,128)S(1)}, f32[512,512]{1,0:T(8,128)}, u32[]{:S(2)}) copy-start(f32[512,512]{1,0:T(8,128)} %get-tuple-element.836) | copy-start | bytes 3145732
  (24 other events, 53.4 us)
Sparse Core Ops, SparseCore 0:
  10.9 63.1 all-gather.6
  94.9 99.6 reduce-scatter.2
  640.8 58.9 all-gather.14
  720.5 94.0 reduce-scatter.4
Sparse Core Ops, SparseCore 1:
  240.0 6.2 all-gather.10
  272.7 7.2 all-gather.8
  578.3 7.5 all-gather.12
  877.6 9.7 all-gather.16
